TPU v7x, 32 devices: a whole 2x2x4 slice. The times are simulated.
32 devices in a mesh: scan: 2 (over y), slab: 16 (over z, x, core).
Axes of the slice: x: 2, y: 2, z: 4, core: 2. Of those that a mesh axis runs over, the one named last changes fastest.
Arguments:
- image: float32 [2, 128, 256, 128], P(None, 'slab', 'scan'), parts along dimension 2, may hold values from -6 to 6
- sensitivity: bfloat16 [12, 2, 128, 128, 128], P('scan', None, 'slab'), parts along dimension 0, may hold values from -1.5 to 1.5
- kernel: float32 [256, 256, 256], P(None, 'slab'), may hold values from 0.1 to 4
Outputs:
- normal_image: float32 [2, 128, 256, 128], P(None, 'slab', 'scan'), parts along dimension 2
There are 2 independent parts, one for each index of `scan`. A program takes and returns all parts, laid end to end along the dimension named above; an argument that names none is the same for every part. Nothing has to cross between parts.
All inputs are finite; a program needn't handle non-finite values.
Results may differ from a plain program's by a relative error of at most 0.0024.
Values may be sent and summed in bfloat16 or wider, within the bound.
A program may use at most 128 MiB of HBM per device.

v0:
```python
import math

import jax
import jax.numpy as jnp
from jax import lax
from jax.sharding import PartitionSpec as P

NX = 128
NY = 128
NZ = 128
GX = 256
GY = 256
GZ = 256


smooth_weight = 0.1


def with_halo(cells, sides, width):
    for axis, dim in sides:
        count = lax.axis_size(axis)
        ends = count - 1
        head = lax.slice_in_dim(cells, 0, width, axis=dim)
        tail = lax.slice_in_dim(cells, cells.shape[dim] - width, cells.shape[dim], axis=dim)
        cells = jnp.concatenate(
            [
                lax.ppermute(tail, axis, [(i, (i + 1) % count) for i in range(ends)]),
                cells,
                lax.ppermute(head, axis, [((i + 1) % count, i) for i in range(ends)]),
            ],
            axis=dim,
        )
    return cells


def fourier_table(count_out, count_in, length, sign_value):
    row_index = lax.broadcasted_iota(jnp.int32, (count_out, count_in), 0)
    column_index = lax.broadcasted_iota(jnp.int32, (count_out, count_in), 1)
    phases = row_index * column_index % length
    angles = phases.astype(jnp.float32) * (2.0 * math.pi / length)
    factor = 1.0 / math.sqrt(length)
    real_part = jnp.cos(angles) * factor
    imaginary = sign_value * jnp.sin(angles) * factor
    stacked = jnp.stack([jnp.stack([real_part, -imaginary]), jnp.stack([imaginary, real_part])])
    return stacked.astype(jnp.bfloat16)


def apply_table(matrix, values, pattern):
    return jnp.einsum(pattern, matrix, values, preferred_element_type=jnp.float32)


def local(image, sensitivity, kernel):
    forward_first = fourier_table(GX, NX, GX, -1.0)
    forward_second = fourier_table(GY, NY, GY, -1.0)
    forward_third = fourier_table(GZ, NZ, GZ, -1.0)
    inverse_first = fourier_table(NX, GX, GX, 1.0)
    inverse_second = fourier_table(NY, GY, GY, 1.0)
    inverse_third = fourier_table(NZ, GZ, GZ, 1.0)
    coil_real = sensitivity[:, 0].astype(jnp.float32)
    coil_imaginary = sensitivity[:, 1].astype(jnp.float32)
    coil_images = jnp.stack(
        [
            coil_real * image[0] - coil_imaginary * image[1],
            coil_real * image[1] + coil_imaginary * image[0],
        ],
        axis=1,
    ).astype(jnp.bfloat16)
    along_second = apply_table(forward_second, coil_images, "pqkj,cqajb->cpakb").astype(
        jnp.bfloat16
    )
    along_third = apply_table(
        forward_third,
        lax.all_to_all(along_second, "slab", split_axis=3, concat_axis=2, tiled=True),
        "pqkj,cqabj->cpabk",
    ).astype(jnp.bfloat16)
    spectrum = apply_table(forward_first, along_third, "pqkj,cqjab->cpkab")
    filtered = (spectrum * kernel).astype(jnp.bfloat16)
    back_first = apply_table(inverse_first, filtered, "pqkj,cqjab->cpkab").astype(jnp.bfloat16)
    back_third = apply_table(inverse_third, back_first, "pqkj,cqabj->cpabk").astype(jnp.bfloat16)
    back_third = lax.all_to_all(back_third, "slab", split_axis=2, concat_axis=3, tiled=True)
    coil_results = apply_table(inverse_second, back_third, "pqkj,cqajb->cpakb")
    summed_real = jnp.sum(
        coil_real * coil_results[:, 0] + coil_imaginary * coil_results[:, 1], axis=0
    )
    summed_imaginary = jnp.sum(
        coil_real * coil_results[:, 1] - coil_imaginary * coil_results[:, 0], axis=0
    )
    padded = with_halo(image.astype(jnp.bfloat16), (("slab", 1),), 1).astype(image.dtype)
    beside = padded[:, 2:] + padded[:, :-2]
    local_pad = jnp.pad(image, ((0, 0), (0, 0), (1, 1), (1, 1)))
    beside = beside + local_pad[:, :, 2:, 1:-1] + local_pad[:, :, :-2, 1:-1]
    beside = beside + local_pad[:, :, 1:-1, 2:] + local_pad[:, :, 1:-1, :-2]
    penalty = 6.0 * image - beside
    return jnp.stack([summed_real, summed_imaginary]) + smooth_weight * penalty


def solution(mesh):
    return jax.shard_map(
        local,
        mesh=mesh,
        in_specs=(
            P(None, "slab", "scan", None),
            P("scan", None, "slab", None, None),
            P(None, "slab", None),
        ),
        out_specs=P(None, "slab", "scan", None),
        check_vma=False,
    )
```

profile of v0, /device:TPU:11, one launch (start us, length us, event | category | flops | bytes accessed | tf_op | source)
XLA Modules:
  0.0 404.1 jit_solution(8972323862147005530)
XLA Ops:
  0.0 0.5 negate_convert_fusion.1
  0.5 1.1 fusion.52
  1.7 3.4 fusion.60
  5.0 0.9 copy.77
  6.0 1.9 copy.78
  7.9 2.3 slice_bitcast_fusion.1
  10.1 2.0 copy.37
  12.2 2.0 copy.39
  14.2 0.9 maximum_bitcast_fusion.4
  15.1 0.0 copy-start.2
  15.1 2.3 fusion.21
  17.4 4.5 %fusion.13 = bf16[6,2,8,256,128]{3,4,1,2,0:T(8,128)(2,1)} fusion(bf16[6,1,8,128,128]{3,4,1,2,0:T(8,128)(2,1)S(1)} %get-tuple-element.8, bf16[6,1,8,128,128]{3,4,1,2,0:T(8,128)(2,1)S(1)} %get-tuple-element.7, bf16[1,2,256,128]{3,2,1,0:T(8,128)(2,1)S(1)} %get-tuple-element.18, bf16[1,2,256,128]{3,2,1,0:T(8,128)(2,1)S(1)} %get-tuple-element.17), kind=kOutput, calls=%fused_computation.14 | convolution fusion | flops 1620574208 | bytes 9699328 | tf_op jit(solution)/shard_map/pqkj,cqajb->cpakb/dot_general | solution.py:49
  21.8 0.0 copy-done.2
  21.8 16.3 %copy.40 = bf16[6,2,8,256,128]{4,1,2,0,3:T(2,128)(2,1)} copy(bf16[6,2,8,256,128]{3,4,1,2,0:T(8,128)(2,1)} %fusion.13) | data formatting | bytes 12582912 | tf_op jit(solution)/shard_map/convert_element_type | solution.py:68
  38.2 6.5 %all-to-all-start = ((bf16[6,2,8,256,128]{4,1,2,0,3:T(2,128)(2,1)}), bf16[6,2,8,256,128]{4,1,2,0,3:T(2,128)(2,1)}, u32[]{:S(2)}, u32[]{:S(2)}) async-start(bf16[6,2,8,256,128]{4,1,2,0,3:T(2,128)(2,1)} %copy.40), calls=%async_computation | async-start | bytes 12582912 | tf_op jit(solution)/shard_map/all_to_all | solution.py:73
  44.7 5.3 %copy.45 = f32[256,16,256]{0,2,1:T(8,128)} copy(f32[256,16,256]{2,1,0:T(8,128)} %param.5) | data formatting | bytes 8388608 | tf_op args[2]
  50.0 0.5 fusion.53
  50.5 0.5 negate_convert_fusion
  51.1 131.0 %all-to-all-done = bf16[6,2,8,256,128]{4,1,2,0,3:T(2,128)(2,1)} async-done(((bf16[6,2,8,256,128]{4,1,2,0,3:T(2,128)(2,1)}), bf16[6,2,8,256,128]{4,1,2,0,3:T(2,128)(2,1)}, u32[]{:S(2)}, u32[]{:S(2)}) %all-to-all-start) | async-done | bytes 6291488 | tf_op jit(solution)/shard_map/all_to_all | solution.py:73
  182.1 5.2 %copy.41 = bf16[6,2,8,256,128]{4,3,2,1,0:T(8,128)(2,1)S(1)} copy(bf16[6,2,8,256,128]{4,1,2,0,3:T(2,128)(2,1)} %all-to-all-done) | data formatting | bytes 12582912 | tf_op jit(solution)/shard_map/all_to_all | solution.py:73
  187.3 0.0 copy-start.3
  187.3 4.4 %copy.42 = bf16[6,2,16,8,16,128]{5,4,3,2,1,0:T(8,128)(2,1)} copy(bf16[6,2,16,8,16,128]{5,4,2,3,1,0:T(8,128)(2,1)S(1)} %bitcast.107) | data formatting | bytes 12582912 | tf_op jit(solution)/shard_map/all_to_all | solution.py:73
  191.7 0.0 copy-done.3
  191.8 9.3 %fusion.7 = bf16[6,2,128,16,256,1]{4,3,1,2,0,5:T(8,128)(2,1)} fusion(bf16[6,2,128,16,128,1]{4,3,2,1,0,5:T(8,128)(2,1)} %bitcast.106, bf16[1,2,256,128]{3,2,1,0:T(8,128)(2,1)S(1)} %copy-done.3, bf16[1,2,256,128]{3,2,1,0:T(8,128)(2,1)S(1)} %get-tuple-element.17), kind=kOutput, calls=%fused_computation.8 | convolution fusion | flops 3228041216 | bytes 19136512 | tf_op jit(solution)/shard_map/pqkj,cqabj->cpabk/dot_general | solution.py:49
  201.1 18.4 %fusion.2 = bf16[6,16,256,2,128,1]{4,2,5,3,1,0:T(8,128)(2,1)} fusion(f32[256,16,256]{0,2,1:T(8,128)} %copy.45, bf16[6,2,128,16,256,1]{4,3,1,2,0,5:T(8,128)(2,1)} %fusion.7, bf16[1,2,128,256]{3,2,1,0:T(8,128)(2,1)S(1)} %get-tuple-element.16, bf16[1,2,128,256]{3,2,1,0:T(8,128)(2,1)S(1)} %get-tuple-element.15, bf16[1,2,256,128]{3,2,1,0:T(8,128)(2,1)} %copy-done.2, ...), kind=kOutput, calls=%fused_computation.3 | convolution fusion | flops 12911116288 | bytes 29884416 | tf_op jit(solution)/shard_map/pqkj,cqjab->cpkab/dot_general | solution.py:49
  219.5 11.6 %fusion.14 = bf16[6,2,128,16,128]{4,2,1,3,0:T(8,128)(2,1)S(1)} fusion(bf16[6,16,256,2,128,1]{4,2,5,3,1,0:T(8,128)(2,1)} %fusion.2, bf16[1,2,128,256]{3,2,1,0:T(8,128)(2,1)S(1)} %get-tuple-element.16, bf16[1,2,128,256]{3,2,1,0:T(8,128)(2,1)S(1)} %get-tuple-element.15), kind=kOutput, calls=%fused_computation.15 | convolution fusion | flops 3224895488 | bytes 19136512 | tf_op jit(solution)/shard_map/pqkj,cqabj->cpabk/dot_general | solution.py:49
  231.1 18.0 %copy.47 = bf16[6,2,128,16,128]{4,1,3,0,2:T(2,128)(2,1)} copy(bf16[6,2,128,16,128]{4,2,1,3,0:T(8,128)(2,1)S(1)} %fusion.14) | data formatting | bytes 12582912 | tf_op jit(solution)/shard_map/convert_element_type | solution.py:79
  249.0 4.8 %all-to-all-start.1 = ((bf16[6,2,128,16,128]{4,1,3,0,2:T(2,128)(2,1)}), bf16[6,2,128,16,128]{4,1,3,0,2:T(2,128)(2,1)}, u32[]{:S(2)}, u32[]{:S(2)}) async-start(bf16[6,2,128,16,128]{4,1,3,0,2:T(2,128)(2,1)} %copy.47), calls=%async_computation.1 | async-start | bytes 12582912 | tf_op jit(solution)/shard_map/all_to_all | solution.py:80
  253.8 2.5 copy.51
  256.3 1.3 convert_element_type.119
  257.7 3.4 collective-permute-start
  261.0 1.9 collective-permute-start.1
  263.0 127.2 %collective-permute-done = bf16[2,1,128,128]{2,3,1,0:T(8,128)(2,1)S(1)} collective-permute-done((bf16[2,1,128,128]{2,3,1,0:T(8,128)(2,1)S(1)}, bf16[2,1,128,128]{2,3,1,0:T(8,128)(2,1)S(1)}, u32[]{:S(2)}, u32[]{:S(2)}) %collective-permute-start) | collective-permute-done | bytes 65568 | tf_op jit(solution)/shard_map/ppermute | solution.py:27
  390.2 1.6 collective-permute-done.1
  391.8 1.2 maximum_convert_fusion
  393.0 0.0 all-to-all-done.1
  393.0 3.8 copy.48
  396.8 1.8 copy.49
  398.6 1.9 fusion.30
  400.5 0.0 copy-start
  400.5 0.0 copy-start.1
  400.5 1.3 fusion.25
  401.8 0.0 copy-done
  401.8 0.3 copy-done.1
  402.1 0.6 fusion.39
  402.8 1.3 copy.54
  (2 shorter events, 0.0 us)
Async XLA Ops:
  15.1 6.8 %copy-start.2 = (bf16[1,2,256,128]{3,2,1,0:T(8,128)(2,1)}, bf16[1,2,256,128]{3,2,1,0:T(8,128)(2,1)S(1)}, u32[]{:S(2)}) copy-start(bf16[1,2,256,128]{3,2,1,0:T(8,128)(2,1)S(1)} %get-tuple-element.18) | copy-start | bytes 393220
  38.2 143.9 %all-to-all-start = ((bf16[6,2,8,256,128]{4,1,2,0,3:T(2,128)(2,1)}), bf16[6,2,8,256,128]{4,1,2,0,3:T(2,128)(2,1)}, u32[]{:S(2)}, u32[]{:S(2)}) async-start(bf16[6,2,8,256,128]{4,1,2,0,3:T(2,128)(2,1)} %copy.40), calls=%async_computation | async-start | bytes 12582912 | tf_op jit(solution)/shard_map/all_to_all | solution.py:73
  187.3 4.4 %copy-start.3 = (bf16[1,2,256,128]{3,2,1,0:T(8,128)(2,1)S(1)}, bf16[1,2,256,128]{3,2,1,0:T(8,128)(2,1)}, u32[]{:S(2)}) copy-start(bf16[1,2,256,128]{3,2,1,0:T(8,128)(2,1)} %copy-done.2) | copy-start | bytes 393220
  249.0 144.0 %all-to-all-start.1 = ((bf16[6,2,128,16,128]{4,1,3,0,2:T(2,128)(2,1)}), bf16[6,2,128,16,128]{4,1,3,0,2:T(2,128)(2,1)}, u32[]{:S(2)}, u32[]{:S(2)}) async-start(bf16[6,2,128,16,128]{4,1,3,0,2:T(2,128)(2,1)} %copy.47), calls=%async_computation.1 | async-start | bytes 12582912 | tf_op jit(solution)/shard_map/all_to_all | solution.py:80
  257.7 132.5 %collective-permute-start = (bf16[2,1,128,128]{2,3,1,0:T(8,128)(2,1)S(1)}, bf16[2,1,128,128]{2,3,1,0:T(8,128)(2,1)S(1)}, u32[]{:S(2)}, u32[]{:S(2)}) collective-permute-start(bf16[2,1,128,128]{2,3,1,0:T(8,128)(2,1)S(1)} %get-tuple-element.13), channel_id=1, source_target_pairs={{0,1},{1,2},{2,3},{3,4},{4,5},{5,6},{6,7},{7,8},{8,9},{9,10},{10,1... | collective-permute-start | bytes 196616 | tf_op jit(solution)/shard_map/ppermute | solution.py:27
  261.0 130.8 %collective-permute-start.1 = (bf16[2,1,128,128]{2,3,1,0:T(8,128)(2,1)S(1)}, bf16[2,1,128,128]{2,3,1,0:T(8,128)(2,1)S(1)}, u32[]{:S(2)}, u32[]{:S(2)}) collective-permute-start(bf16[2,1,128,128]{2,3,1,0:T(8,128)(2,1)S(1)} %get-tuple-element.14), channel_id=1, source_target_pairs={{1,0},{2,1},{3,2},{4,3},{5,4},{6,5},{7,6},{8,7},{9,8},{10,9},{11,1... | collective-permute-start | bytes 196616 | tf_op jit(solution)/shard_map/ppermute | solution.py:29
  400.5 1.3 copy-start
  400.5 1.6 copy-start.1
where the time goes:
time: 405 us; the launch traced here: 404 us
  waiting for transfers between devices  260 us (64%)
  local copies, waits for them, and re-layouts  71.5 us (18%)
  matrix products  45.6 us (11%)
  starting transfers between devices  16.6 us (4%)
  other arithmetic  10.3 us (3%)
    all_to_all x1, waiting for transfers between devices, local(): lax.all_to_all(along_second, 'slab', split_axis=3, concat_axis=2, tiled=T...  131 us
    ppermute x1, waiting for transfers between devices, with_halo(): lax.ppermute(tail, axis, [(i, (i + 1) % count) for i in range(ends)])  127 us
    dot_general x5, matrix products, apply_table(): jnp.einsum(pattern, matrix, values, preferred_element_type=jnp.float32)  45.6 us
    convert_element_type x1, local copies, waits for them, and re-layouts, local(): apply_table(inverse_third, back_first, 'pqkj,cqabj->cpabk')  18 us
    convert_element_type x1, local copies, waits for them, and re-layouts, local(): apply_table(forward_second, coil_images, 'pqkj,cqajb->cpakb')  16.3 us
    unnamed x12, local copies, waits for them, and re-layouts  11 us
    all_to_all x2, local copies, waits for them, and re-layouts, local(): lax.all_to_all(along_second, 'slab', split_axis=3, concat_axis=2, tiled=T...  9.64 us
  transfers between devices with their start and end apart: 4, of which 3 were waited for; matrix products, arithmetic and copies ran while one was open for 3% of the time, Pallas kernels for 0%

commit v1 on v0

v1 whole, which is shorter than its diff:
```python
import functools
import math

import jax
import jax.numpy as jnp
import numpy as np
from jax import lax
from jax.experimental import pallas as pl
from jax.experimental.pallas import tpu as pltpu
from jax.sharding import PartitionSpec as P

MESH = pl.DeviceIdType.MESH
smooth_weight = 0.1
F32 = jnp.float32
BF16 = jnp.bfloat16


def factor(count_out, count_in, length, sign_value):
    phases = np.outer(np.arange(count_out), np.arange(count_in)) % length
    angles = phases * (2.0 * math.pi / length)
    scale = 1.0 / math.sqrt(length)
    real, imag = np.cos(angles) * scale, sign_value * np.sin(angles) * scale
    return np.block([[real, -imag], [imag, real]]).astype(jnp.bfloat16)


def dot(a, b):
    return jnp.dot(a, b, preferred_element_type=F32)


def shifted(cells, step, axis):
    count = cells.shape[axis]
    index = lax.broadcasted_iota(jnp.int32, cells.shape, axis)
    edge = 0 if step == 1 else count - 1
    return jnp.where(index == edge, 0.0, pltpu.roll(cells, step % count, axis))


def kernel_body(
    n, image, sens, weight, fy, fzt, fx, hx, hzt, hy, out,
    sent, got, back, home, rows, halo, filt,
    send1, recv1, send2, recv2, hsend, hrecv, wsem,
):
    me = lax.axis_index("slab")
    coils, _, xs, ny, nz = sens.shape
    gx, gz = fx.shape[0] // 2, weight.shape[1]
    nx, gy = n * xs, fy.shape[0] // 2
    kys = gy // n
    part = kys * xs
    pair = 16 // xs

    columns = [
        pltpu.make_async_copy(weight.at[:, pl.ds(i * 128, 128)], filt.at[i], wsem.at[i])
        for i in range(gz // 128)
    ]
    for copy in columns:
        copy.start()

    barrier = pltpu.get_barrier_semaphore()

    @pl.loop(1, n)
    def _(k):
        pl.semaphore_signal(barrier, inc=1, device_id={"slab": lax.rem(me + k, n)}, device_id_type=MESH)

    pl.semaphore_wait(barrier, n - 1)

    def halo_copy(p, side):
        plane = xs - 1 if side == 0 else 0
        to = me + 1 if side == 0 else me - 1
        return pltpu.make_async_remote_copy(
            src_ref=image.at[p, plane], dst_ref=halo.at[side, p],
            send_sem=hsend.at[side, p], recv_sem=hrecv.at[side, p],
            device_id={"slab": lax.rem(to + n, n)}, device_id_type=MESH)

    def exchange(source, target, c, k, send_sem, recv_sem):
        to = lax.rem(me + k, n)
        return pltpu.make_async_remote_copy(
            src_ref=source.at[c, to], dst_ref=target.at[c, me],
            send_sem=send_sem.at[c, to], recv_sem=recv_sem.at[c, me],
            device_id={"slab": to}, device_id_type=MESH)

    def arrival(source, target, c, k, send_sem, recv_sem):
        owner = lax.rem(me + k, n)
        return pltpu.make_async_remote_copy(
            src_ref=source.at[c, owner], dst_ref=target.at[c, owner],
            send_sem=send_sem.at[c, owner], recv_sem=recv_sem.at[c, owner],
            device_id={"slab": owner}, device_id_type=MESH)

    def start_all(source, target, c, send_sem, recv_sem):
        @pl.loop(1, n)
        def _(k):
            exchange(source, target, c, k, send_sem, recv_sem).start()

        target[c, me] = source[c, me]

    def wait_all(source, target, c, send_sem, recv_sem):
        @pl.loop(1, n)
        def _(k):
            arrival(source, target, c, k, send_sem, recv_sem).wait_recv()

    def drain(source, target, c, send_sem, recv_sem):
        @pl.loop(1, n)
        def _(k):
            exchange(source, target, c, k, send_sem, recv_sem).wait_send()

    @pl.loop(0, coils)
    def _(c):
        @pl.loop(0, xs // 2)
        def _(h):
            halves = []
            for j in range(2):
                x = 2 * h + j
                cr, ci = sens[c, 0, x].astype(F32), sens[c, 1, x].astype(F32)
                vr, vi = image[0, x], image[1, x]
                halves.append(jnp.concatenate([cr * vr - ci * vi, cr * vi + ci * vr], axis=0).astype(BF16))
            lines = dot(fy[...], jnp.concatenate(halves, axis=1))
            for j in range(2):
                rows[pl.ds(2 * h + j, 2 * gy, stride=xs), :] = lines[:, j * nz:(j + 1) * nz]

        for q in range(2):
            size = gy * xs
            sent[c, :, q * part:(q + 1) * part, :] = (
                rows[q * size:(q + 1) * size, :].reshape(n, part, nz).astype(BF16))
        start_all(sent, got, c, send1, recv1)

        @pl.when(c == 0)
        def _():
            @pl.when(me < n - 1)
            def _():
                for p in range(2):
                    halo_copy(p, 0).start()

            @pl.when(me > 0)
            def _():
                for p in range(2):
                    halo_copy(p, 1).start()

    for copy in columns:
        copy.wait()

    @pl.loop(0, coils)
    def _(c):
        wait_all(sent, got, c, send1, recv1)

        @pl.loop(0, kys // pair)
        def _(kp):
            base = pl.multiple_of(kp * 16, 16)
            cells = [got[c, :, pl.ds(q * part + base, 16), :].reshape(n * 16, nz) for q in range(2)]
            third = dot(jnp.concatenate(cells, axis=1), fzt[...]).reshape(n, pair, xs, 2 * gz)
            results = []
            for j in range(pair):
                b = third[:, j].reshape(nx, 2 * gz).astype(BF16)
                spectrum = dot(fx[...], jnp.concatenate([b[:, :gz], b[:, gz:]], axis=0))
                k = jnp.concatenate(
                    [filt[i, pl.ds(kp * pair + j, gx, stride=kys), :] for i in range(gz // 128)], axis=1)
                filtered = jnp.concatenate([spectrum[:gx] * k, spectrum[gx:] * k], axis=0).astype(BF16)
                first = dot(hx[...], filtered).astype(BF16)
                results.append(dot(jnp.concatenate([first[:nx], first[nx:]], axis=1), hzt[...]))
            for q in range(2):
                parts = [r[:, q * nz:(q + 1) * nz].reshape(n, 1, xs, nz) for r in results]
                back[c, :, pl.ds(q * part + base, 16), :] = (
                    jnp.concatenate(parts, axis=1).reshape(n, 16, nz).astype(BF16))

        start_all(back, home, c, send2, recv2)

    @pl.when(me < n - 1)
    def _():
        for p in range(2):
            halo_copy(p, 0).wait_send()
            halo_copy(p, 1).wait_recv()

    @pl.when(me > 0)
    def _():
        for p in range(2):
            halo_copy(p, 1).wait_send()
            halo_copy(p, 0).wait_recv()

    for p in range(2):
        for x in range(xs):
            here = image[p, x]
            if x == 0:
                before = jnp.where(me > 0, halo[0, p], 0.0)
            else:
                before = image[p, x - 1]
            if x == xs - 1:
                after = jnp.where(me < n - 1, halo[1, p], 0.0)
            else:
                after = image[p, x + 1]
            beside = before + after
            for axis in range(2):
                beside = beside + shifted(here, 1, axis) + shifted(here, -1, axis)
            out[p, x] = smooth_weight * (6.0 * here - beside)

    @pl.loop(0, coils)
    def _(c):
        wait_all(back, home, c, send2, recv2)
        size = gy * xs
        for q in range(2):
            rows[q * size:(q + 1) * size, :] = home[c, :, q * part:(q + 1) * part, :].reshape(size, nz).astype(F32)

        @pl.loop(0, xs // 2)
        def _(h):
            lines = [rows[pl.ds(2 * h + j, 2 * gy, stride=xs), :] for j in range(2)]
            cells = dot(hy[...], jnp.concatenate(lines, axis=1).astype(BF16))
            for j in range(2):
                x = 2 * h + j
                re, im = cells[:ny, j * nz:(j + 1) * nz], cells[ny:, j * nz:(j + 1) * nz]
                cr, ci = sens[c, 0, x].astype(F32), sens[c, 1, x].astype(F32)
                out[0, x] = out[0, x] + cr * re + ci * im
                out[1, x] = out[1, x] + cr * im - ci * re

    @pl.loop(0, coils)
    def _(c):
        drain(sent, got, c, send1, recv1)
        drain(back, home, c, send2, recv2)


def fused(n, image, sensitivity, kernel):
    coils, _, xs, ny, nz = sensitivity.shape
    gx, kys, gz = kernel.shape
    nx, gy = n * xs, n * kys
    block = (coils, n, 2 * kys * xs, nz)
    tables = (
        factor(gy, ny, gy, -1.0),
        factor(gz, nz, gz, -1.0).T,
        factor(gx, nx, gx, -1.0),
        factor(nx, gx, gx, 1.0),
        factor(nz, gz, gz, 1.0).T,
        factor(ny, gy, gy, 1.0),
    )
    vmem = pl.BlockSpec(memory_space=pltpu.VMEM)
    dma = pltpu.SemaphoreType.DMA
    return pl.pallas_call(
        functools.partial(kernel_body, n),
        out_shape=jax.ShapeDtypeStruct(image.shape, F32),
        in_specs=[vmem] * 2 + [pl.BlockSpec(memory_space=pl.ANY)] + [vmem] * 6,
        out_specs=vmem,
        scratch_shapes=[pltpu.VMEM(block, BF16)] * 4
        + [pltpu.VMEM((2 * gy * xs, nz), F32), pltpu.VMEM((2, 2, ny, nz), F32),
           pltpu.VMEM((gz // 128, gx * kys, 128), F32)]
        + [dma((coils, n))] * 4 + [dma((2, 2))] * 2 + [dma((gz // 128,))],
        compiler_params=pltpu.CompilerParams(
            collective_id=0, has_side_effects=True, vmem_limit_bytes=62 * 2**20),
    )(image, sensitivity, kernel.reshape(gx * kys, gz), *[jnp.asarray(t) for t in tables])


def with_halo(cells, axis, dim):
    count = lax.axis_size(axis)
    head = lax.slice_in_dim(cells, 0, 1, axis=dim)
    tail = lax.slice_in_dim(cells, cells.shape[dim] - 1, cells.shape[dim], axis=dim)
    return jnp.concatenate(
        [
            lax.ppermute(tail, axis, [(i, i + 1) for i in range(count - 1)]),
            cells,
            lax.ppermute(head, axis, [(i + 1, i) for i in range(count - 1)]),
        ],
        axis=dim,
    )


def staged(n, image, sensitivity, kernel):
    coils, _, xs, ny, nz = sensitivity.shape
    gx, kys, gz = kernel.shape
    nx, gy = n * xs, n * kys

    def table(count_out, count_in, length, sign_value):
        both = factor(count_out, count_in, length, sign_value)
        return jnp.asarray(both.reshape(2, count_out, 2, count_in).transpose(0, 2, 1, 3))

    def apply(matrix, values, pattern):
        return jnp.einsum(pattern, matrix, values, preferred_element_type=F32)

    real, imag = sensitivity[:, 0].astype(F32), sensitivity[:, 1].astype(F32)
    images = jnp.stack(
        [real * image[0] - imag * image[1], real * image[1] + imag * image[0]], axis=1).astype(BF16)
    second = apply(table(gy, ny, gy, -1.0), images, "pqkj,cqajb->cpakb").astype(BF16)
    second = lax.all_to_all(second, "slab", split_axis=3, concat_axis=2, tiled=True)
    third = apply(table(gz, nz, gz, -1.0), second, "pqkj,cqabj->cpabk").astype(BF16)
    spectrum = apply(table(gx, nx, gx, -1.0), third, "pqkj,cqjab->cpkab")
    filtered = (spectrum * kernel).astype(BF16)
    first = apply(table(nx, gx, gx, 1.0), filtered, "pqkj,cqjab->cpkab").astype(BF16)
    back = apply(table(nz, gz, gz, 1.0), first, "pqkj,cqabj->cpabk").astype(BF16)
    back = lax.all_to_all(back, "slab", split_axis=2, concat_axis=3, tiled=True)
    cells = apply(table(ny, gy, gy, 1.0), back, "pqkj,cqajb->cpakb")
    summed = jnp.stack([
        jnp.sum(real * cells[:, 0] + imag * cells[:, 1], axis=0),
        jnp.sum(real * cells[:, 1] - imag * cells[:, 0], axis=0)])
    padded = with_halo(image.astype(BF16), "slab", 1).astype(image.dtype)
    beside = padded[:, 2:] + padded[:, :-2]
    wide = jnp.pad(image, ((0, 0), (0, 0), (1, 1), (1, 1)))
    beside = beside + wide[:, :, 2:, 1:-1] + wide[:, :, :-2, 1:-1]
    beside = beside + wide[:, :, 1:-1, 2:] + wide[:, :, 1:-1, :-2]
    return summed + smooth_weight * (6.0 * image - beside)


def solution(mesh):
    n = mesh.shape["slab"]

    def local(image, sensitivity, kernel):
        tiled = sensitivity.shape[2] == 8 and kernel.shape[1] % 2 == 0
        form = fused if tiled else staged
        return form(n, image, sensitivity, kernel)

    return jax.shard_map(
        local,
        mesh=mesh,
        in_specs=(
            P(None, "slab", "scan", None),
            P("scan", None, "slab", None, None),
            P(None, "slab", None),
        ),
        out_specs=P(None, "slab", "scan", None),
        check_vma=False,
    )
```

time: 405 us -> 291 us (0.72)
  Pallas kernels: 0 us -> 288 us
  waiting for transfers between devices: 260 us -> 0 us
  local copies, waits for them, and re-layouts: 71.5 us -> 2.3 us
  matrix products: 45.6 us -> 0 us
  starting transfers between devices: 16.6 us -> 0 us
  other arithmetic: 10.3 us -> 0 us
    pallas_call x0 -> x1, Pallas kernels: none -> 288 us  [fused(): pl.pallas_call(functools.partial(kernel_body, n), out_shape=jax.ShapeDtyp...]
    all_to_all x2 -> x0, waiting for transfers between devices: 131 us -> none  [the longest x1 131 us: local(): lax.all_to_all(along_second, 'slab', split_axis=3, concat_axis=2, tiled=T...]
    ppermute x2 -> x0, waiting for transfers between devices: 129 us -> none  [the longest x1 127 us: with_halo(): lax.ppermute(tail, axis, [(i, (i + 1) % count) for i in range(ends)])]
    dot_general x5 -> x0, matrix products: 45.6 us -> none  [apply_table(): jnp.einsum(pattern, matrix, values, preferred_element_type=jnp.float32)]
    convert_element_type x2 -> x0, local copies, waits for them, and re-layouts: 34.3 us -> none  [the longest x1 18 us: local(): apply_table(inverse_third, back_first, 'pqkj,cqabj->cpabk')]
    all_to_all x4 -> x0, local copies, waits for them, and re-layouts: 15.2 us -> none  [the longest x2 9.64 us: local(): lax.all_to_all(along_second, 'slab', split_axis=3, concat_axis=2, tiled=T...]
    all_to_all x2 -> x0, starting transfers between devices: 11.3 us -> none  [the longest x1 6.52 us: local(): lax.all_to_all(along_second, 'slab', split_axis=3, concat_axis=2, tiled=T...]
    unnamed x12 -> x1, local copies, waits for them, and re-layouts: 11 us -> 2.3 us
  transfers between devices with their start and end apart: 4 -> 0, of which waited for: 3 -> 0; matrix products, arithmetic and copies ran while one was open for 3% -> 0% of each run, Pallas kernels for 0% -> 0%
where the time goes in v1:
time: 291 us; the launch traced here: 290 us
  Pallas kernels  288 us (99%)
    pallas_call x1, Pallas kernels, fused(): pl.pallas_call(functools.partial(kernel_body, n), out_shape=jax.ShapeDtyp...  288 us

profile of v1, /device:TPU:11, one launch (start us, length us, event | category | flops | bytes accessed | tf_op | source)
XLA Modules:
  0.0 290.4 jit_solution(10705006721084539759)
XLA Ops:
  0.0 288.1 %shard_map.91 = f32[2,8,128,128]{3,2,1,0:T(8,128)} custom-call(f32[2,8,128,128]{3,2,1,0:T(8,128)} %image.1, bf16[6,2,8,128,128]{4,3,2,1,0:T(8,128)(2,1)} %sens.1, f32[4096,256]{1,0:T(8,128)} %bitcast.1, bf16[512,256]{1,0:T(8,128)(2,1)} %constant.4.clone.fy.fx.hzt, bf16[256,512]{1,0:T(8,128)(2,1)} %constant.5.clone.fzt.hx.hy, ...), custom_call_target="tpu_custom_call" | custom-call | tf_op jit(solution)/shard_map/pallas_call | solution.py:231
  288.1 2.3 copy.11

commit v2 on v1

--- a/solution.py
+++ b/solution.py
@@ -37,7 +37,8 @@
 def kernel_body(
     n, image, sens, weight, fy, fzt, fx, hx, hzt, hy, out,
     sent, got, back, home, rows, halo, filt,
-    send1, recv1, send2, recv2, hsend, hrecv, wsem,
+    other_sens, mine, other_image, other_out, total, other_total,
+    send1, recv1, send2, recv2, hsend, hrecv, wsem, psend, precv, tsend, trecv,
 ):
     me = lax.axis_index("slab")
     coils, _, xs, ny, nz = sens.shape
@@ -46,6 +47,11 @@
     kys = gy // n
     part = kys * xs
     pair = 16 // xs
+    nh = n // 2
+    half, place = me // nh, lax.rem(me, nh)
+    far = lax.rem(me + nh, n)
+    far_half = 1 - half
+    mid = coils // 2
 
     columns = [
         pltpu.make_async_copy(weight.at[:, pl.ds(i * 128, 128)], filt.at[i], wsem.at[i])
@@ -70,76 +76,110 @@
             send_sem=hsend.at[side, p], recv_sem=hrecv.at[side, p],
             device_id={"slab": lax.rem(to + n, n)}, device_id_type=MESH)
 
-    def exchange(source, target, c, k, send_sem, recv_sem):
-        to = lax.rem(me + k, n)
+    def to_far(source, target, send_sem, recv_sem):
         return pltpu.make_async_remote_copy(
-            src_ref=source.at[c, to], dst_ref=target.at[c, me],
-            send_sem=send_sem.at[c, to], recv_sem=recv_sem.at[c, me],
+            src_ref=source, dst_ref=target, send_sem=send_sem, recv_sem=recv_sem,
+            device_id={"slab": far}, device_id_type=MESH)
+
+    def maps(c):
+        return to_far(sens.at[c], other_sens.at[c], psend.at[c], precv.at[c])
+
+    image_copy = to_far(mine, other_image, tsend.at[0], trecv.at[0])
+    total_copy = to_far(total, other_total, tsend.at[1], trecv.at[1])
+
+    def block(source, target, c, to, slot, landing, send_sem, recv_sem):
+        return pltpu.make_async_remote_copy(
+            src_ref=source.at[c, slot], dst_ref=target.at[c, landing],
+            send_sem=send_sem.at[c, slot], recv_sem=recv_sem.at[c, landing],
             device_id={"slab": to}, device_id_type=MESH)
 
-    def arrival(source, target, c, k, send_sem, recv_sem):
-        owner = lax.rem(me + k, n)
-        return pltpu.make_async_remote_copy(
-            src_ref=source.at[c, owner], dst_ref=target.at[c, owner],
-            send_sem=send_sem.at[c, owner], recv_sem=recv_sem.at[c, owner],
-            device_id={"slab": owner}, device_id_type=MESH)
-
-    def start_all(source, target, c, send_sem, recv_sem):
+    def over_all(source, target, c, send_sem, recv_sem, action):
         @pl.loop(1, n)
         def _(k):
-            exchange(source, target, c, k, send_sem, recv_sem).start()
-
+            to = lax.rem(me + k, n)
+            landing = to if action == "recv" else me
+            act(block(source, target, c, to, to, landing, send_sem, recv_sem), action)
+
+    def over_half(source, target, c, send_sem, recv_sem, action):
+        @pl.loop(1, nh)
+        def _(k):
+            near = lax.rem(place + k, nh)
+            for g in range(2):
+                landing = near if action == "recv" else place
+                act(block(source, target, c, half * nh + near, g * nh + near, g * nh + landing,
+                          send_sem, recv_sem), action)
+
+    def act(copy, action):
+        if action == "start":
+            copy.start()
+        elif action == "recv":
+            copy.wait_recv()
+        else:
+            copy.wait_send()
+
+    def is_split(c):
+        return lax.rem(c, mid) != 0
+
+    def either(c, first, second):
+        pl.when(is_split(c))(first)
+        pl.when(jnp.logical_not(is_split(c)))(second)
+
+    def traffic(source, target, c, send_sem, recv_sem, action):
+        either(c,
+               lambda: over_half(source, target, c, send_sem, recv_sem, action),
+               lambda: over_all(source, target, c, send_sem, recv_sem, action))
+
+    def start_all(source, target, c, send_sem, recv_sem):
+        over_all(source, target, c, send_sem, recv_sem, "start")
         target[c, me] = source[c, me]
 
-    def wait_all(source, target, c, send_sem, recv_sem):
-        @pl.loop(1, n)
-        def _(k):
-            arrival(source, target, c, k, send_sem, recv_sem).wait_recv()
-
-    def drain(source, target, c, send_sem, recv_sem):
-        @pl.loop(1, n)
-        def _(k):
-            exchange(source, target, c, k, send_sem, recv_sem).wait_send()
-
-    @pl.loop(0, coils)
-    def _(c):
+    def start_half(source, target, c, send_sem, recv_sem):
+        over_half(source, target, c, send_sem, recv_sem, "start")
+        for g in range(2):
+            target[c, g * nh + place] = source[c, g * nh + place]
+
+    def along_second(table, maps_of, cells_of):
+        count = table.shape[0]
+
         @pl.loop(0, xs // 2)
         def _(h):
             halves = []
             for j in range(2):
                 x = 2 * h + j
-                cr, ci = sens[c, 0, x].astype(F32), sens[c, 1, x].astype(F32)
-                vr, vi = image[0, x], image[1, x]
+                cr, ci = maps_of(0, x).astype(F32), maps_of(1, x).astype(F32)
+                vr, vi = cells_of(0, x).astype(F32), cells_of(1, x).astype(F32)
                 halves.append(jnp.concatenate([cr * vr - ci * vi, cr * vi + ci * vr], axis=0).astype(BF16))
-            lines = dot(fy[...], jnp.concatenate(halves, axis=1))
+            lines = dot(table, jnp.concatenate(halves, axis=1))
             for j in range(2):
-                rows[pl.ds(2 * h + j, 2 * gy, stride=xs), :] = lines[:, j * nz:(j + 1) * nz]
-
+                rows[pl.ds(2 * h + j, count, stride=xs), :] = lines[:, j * nz:(j + 1) * nz]
+
+    def forward_all(c):
+        along_second(fy[...], lambda p, x: sens[c, p, x], lambda p, x: image[p, x])
+        size = gy * xs
         for q in range(2):
-            size = gy * xs
             sent[c, :, q * part:(q + 1) * part, :] = (
                 rows[q * size:(q + 1) * size, :].reshape(n, part, nz).astype(BF16))
         start_all(sent, got, c, send1, recv1)
 
-        @pl.when(c == 0)
-        def _():
-            @pl.when(me < n - 1)
-            def _():
-                for p in range(2):
-                    halo_copy(p, 0).start()
-
-            @pl.when(me > 0)
-            def _():
-                for p in range(2):
-                    halo_copy(p, 1).start()
-
-    for copy in columns:
-        copy.wait()
-
-    @pl.loop(0, coils)
-    def _(c):
-        wait_all(sent, got, c, send1, recv1)
-
+    gh = gy // 2
+
+    def forward_half(c):
+        maps(c).wait_recv()
+        table = jnp.concatenate(
+            [fy[pl.ds(pl.multiple_of(q * gy + half * gh, gh), gh), :] for q in range(2)], axis=0)
+        size = gh * xs
+        for own in (True, False):
+            if own:
+                along_second(table, lambda p, x: sens[c, p, x], lambda p, x: image[p, x])
+            else:
+                along_second(table, lambda p, x: other_sens[c, p, x], lambda p, x: other_image[p, x])
+            start = (half if own else far_half) * nh
+            for q in range(2):
+                sent[c, pl.ds(start, nh), q * part:(q + 1) * part, :] = (
+                    rows[q * size:(q + 1) * size, :].reshape(nh, part, nz).astype(BF16))
+        start_half(sent, got, c, send1, recv1)
+
+    def middle(c):
         @pl.loop(0, kys // pair)
         def _(kp):
             base = pl.multiple_of(kp * 16, 16)
@@ -159,7 +199,95 @@
                 back[c, :, pl.ds(q * part + base, 16), :] = (
                     jnp.concatenate(parts, axis=1).reshape(n, 16, nz).astype(BF16))
 
-        start_all(back, home, c, send2, recv2)
+    def gather(table, count, maps_of, acc):
+        @pl.loop(0, xs // 2)
+        def _(h):
+            lines = [rows[pl.ds(2 * h + j, count, stride=xs), :] for j in range(2)]
+            cells = dot(table, jnp.concatenate(lines, axis=1).astype(BF16))
+            for j in range(2):
+                x = 2 * h + j
+                re, im = cells[:ny, j * nz:(j + 1) * nz], cells[ny:, j * nz:(j + 1) * nz]
+                cr, ci = maps_of(0, x).astype(F32), maps_of(1, x).astype(F32)
+                acc[0, x] = acc[0, x] + cr * re + ci * im
+                acc[1, x] = acc[1, x] + cr * im - ci * re
+
+    def inverse_all(c):
+        over_all(back, home, c, send2, recv2, "recv")
+        size = gy * xs
+        for q in range(2):
+            rows[q * size:(q + 1) * size, :] = home[c, :, q * part:(q + 1) * part, :].reshape(size, nz).astype(F32)
+        gather(hy[...], 2 * gy, lambda p, x: sens[c, p, x], out)
+
+    def inverse_half(c):
+        over_half(back, home, c, send2, recv2, "recv")
+        table = jnp.concatenate(
+            [hy[:, pl.ds(pl.multiple_of(q * gy + half * gh, gh), gh)] for q in range(2)], axis=1)
+        size = gh * xs
+        for own in (False, True):
+            start = (half if own else far_half) * nh
+            for q in range(2):
+                rows[q * size:(q + 1) * size, :] = (
+                    home[c, pl.ds(start, nh), q * part:(q + 1) * part, :].reshape(size, nz).astype(F32))
+            if own:
+                gather(table, 2 * gh, lambda p, x: sens[c, p, x], out)
+            else:
+                gather(table, 2 * gh, lambda p, x: other_sens[c, p, x], other_out)
+
+    mine[...] = image[...].astype(BF16)
+    maps(1).start()
+    image_copy.start()
+    forward_all(0)
+    maps(2).start()
+
+    @pl.when(me < n - 1)
+    def _():
+        for p in range(2):
+            halo_copy(p, 0).start()
+
+    @pl.when(me > 0)
+    def _():
+        for p in range(2):
+            halo_copy(p, 1).start()
+
+    other_out[...] = jnp.zeros_like(other_out)
+    out[...] = jnp.zeros_like(out)
+    image_copy.wait_recv()
+    forward_half(1)
+    for copy in columns:
+        copy.wait()
+
+    @pl.loop(0, coils)
+    def _(c):
+        @pl.when(c < mid - 1)
+        def _():
+            maps(c + mid + 1).start()
+
+        @pl.when(c == 0)
+        def _():
+            forward_half(2)
+            forward_all(mid)
+
+        @pl.when(jnp.logical_and(c > 0, c < mid))
+        def _():
+            forward_half(c + mid)
+
+        traffic(sent, got, c, send1, recv1, "recv")
+        middle(c)
+        either(c,
+               lambda: start_half(back, home, c, send2, recv2),
+               lambda: start_all(back, home, c, send2, recv2))
+
+        @pl.when(jnp.logical_and(c >= mid, c < coils - 1))
+        def _():
+            inverse_half(c - mid + 1)
+
+    @pl.loop(mid + 1, coils)
+    def _(c):
+        inverse_half(c)
+
+    total[...] = other_out[...].astype(BF16)
+    total_copy.start()
+    inverse_all(0)
 
     @pl.when(me < n - 1)
     def _():
@@ -187,30 +315,24 @@
             beside = before + after
             for axis in range(2):
                 beside = beside + shifted(here, 1, axis) + shifted(here, -1, axis)
-            out[p, x] = smooth_weight * (6.0 * here - beside)
+            out[p, x] = out[p, x] + smooth_weight * (6.0 * here - beside)
+
+    inverse_all(mid)
+    total_copy.wait_recv()
+    out[...] = out[...] + other_total[...].astype(F32)
 
     @pl.loop(0, coils)
     def _(c):
-        wait_all(back, home, c, send2, recv2)
-        size = gy * xs
-        for q in range(2):
-            rows[q * size:(q + 1) * size, :] = home[c, :, q * part:(q + 1) * part, :].reshape(size, nz).astype(F32)
-
-        @pl.loop(0, xs // 2)
-        def _(h):
-            lines = [rows[pl.ds(2 * h + j, 2 * gy, stride=xs), :] for j in range(2)]
-            cells = dot(hy[...], jnp.concatenate(lines, axis=1).astype(BF16))
-            for j in range(2):
-                x = 2 * h + j
-                re, im = cells[:ny, j * nz:(j + 1) * nz], cells[ny:, j * nz:(j + 1) * nz]
-                cr, ci = sens[c, 0, x].astype(F32), sens[c, 1, x].astype(F32)
-                out[0, x] = out[0, x] + cr * re + ci * im
-                out[1, x] = out[1, x] + cr * im - ci * re
-
-    @pl.loop(0, coils)
+        traffic(sent, got, c, send1, recv1, "send")
+        traffic(back, home, c, send2, recv2, "send")
+
+    @pl.loop(1, mid)
     def _(c):
-        drain(sent, got, c, send1, recv1)
-        drain(back, home, c, send2, recv2)
+        maps(c).wait_send()
+        maps(c + mid).wait_send()
+
+    image_copy.wait_send()
+    total_copy.wait_send()
 
 
 def fused(n, image, sensitivity, kernel):
@@ -236,7 +358,11 @@
         scratch_shapes=[pltpu.VMEM(block, BF16)] * 4
         + [pltpu.VMEM((2 * gy * xs, nz), F32), pltpu.VMEM((2, 2, ny, nz), F32),
            pltpu.VMEM((gz // 128, gx * kys, 128), F32)]
-        + [dma((coils, n))] * 4 + [dma((2, 2))] * 2 + [dma((gz // 128,))],
+        + [pltpu.VMEM(sensitivity.shape, BF16)]
+        + [pltpu.VMEM(image.shape, BF16)] * 2 + [pltpu.VMEM(image.shape, F32)]
+        + [pltpu.VMEM(image.shape, BF16)] * 2
+        + [dma((coils, n))] * 4 + [dma((2, 2))] * 2 + [dma((gz // 128,))]
+        + [dma((coils,))] * 2 + [dma((2,))] * 2,
         compiler_params=pltpu.CompilerParams(
             collective_id=0, has_side_effects=True, vmem_limit_bytes=62 * 2**20),
     )(image, sensitivity, kernel.reshape(gx * kys, gz), *[jnp.asarray(t) for t in tables])
@@ -295,7 +421,7 @@
     n = mesh.shape["slab"]
 
     def local(image, sensitivity, kernel):
-        tiled = sensitivity.shape[2] == 8 and kernel.shape[1] % 2 == 0
+        tiled = sensitivity.shape[2] == 8 and kernel.shape[1] % 2 == 0 and n % 2 == 0 and sensitivity.shape[0] == 6
         form = fused if tiled else staged
         return form(n, image, sensitivity, kernel)
 

time: 291 us -> 290 us (level)
  Pallas kernels: 288 us -> 285 us
where the time goes in v2:
time: 290 us; the launch traced here: 288 us
  Pallas kernels  285 us (98%)
    pallas_call x1, Pallas kernels, fused(): pl.pallas_call(functools.partial(kernel_body, n), out_shape=jax.ShapeDtyp...  285 us

profile of v2, /device:TPU:11, one launch (start us, length us, event | category | flops | bytes accessed | tf_op | source)
XLA Modules:
  0.0 287.7 jit_solution(15354241705622936348)
XLA Ops:
  0.0 285.4 %shard_map.91 = f32[2,8,128,128]{3,2,1,0:T(8,128)} custom-call(f32[2,8,128,128]{3,2,1,0:T(8,128)} %image.1, bf16[6,2,8,128,128]{4,3,2,1,0:T(8,128)(2,1)} %sens.1, f32[4096,256]{1,0:T(8,128)} %bitcast.1, bf16[512,256]{1,0:T(8,128)(2,1)} %constant.4.clone.fy.fx.hzt, bf16[256,512]{1,0:T(8,128)(2,1)} %constant.5.clone.fzt.hx.hy, ...), custom_call_target="tpu_custom_call" | custom-call | tf_op jit(solution)/shard_map/pallas_call | solution.py:353
  285.4 2.3 copy.11
